TPU v7x, 256 devices: a whole 4x4x8 slice. The times are simulated.
256 devices in a mesh: blk: 256 (over y, z, x, core).
Axes of the slice: x: 4, y: 4, z: 8, core: 2. Of those that a mesh axis runs over, the one named last changes fastest.
Arguments:
- image_features: bfloat16 [65536, 1536], P('blk'), may hold values from -0.5 to 0.5
- head_weight: bfloat16 [1536, 1152], P('blk'), may hold values from -0.15625 to 0.15625
- text_embeds: bfloat16 [65536, 1152], P('blk'), may hold values from -0.29882812 to 0.29882812
- natural_exponent_factor: float32 [1], replicated, may hold values from 1.6 to 2.6
- logit_bias: float32 [1], replicated, may hold values from -4 to -1
Outputs:
- grad_features: bfloat16 [65536, 1536], P('blk')
- grad_text: bfloat16 [65536, 1152], P('blk')
- grad_weight: float32 [1536, 1152], P('blk')
All inputs are finite; a program needn't handle non-finite values.
Results may differ from a plain program's by a relative error of at most 0.0085.
Values may be sent and summed in bfloat16 or wider, within the bound.
No kernel may reach another device: no remote copies, remote signals or barrier semaphores. Data moves between devices by JAX's collectives and lax.ppermute only.
A program may use at most 64 MiB of HBM per device.

v0:
```python
import jax
import jax.numpy as jnp
from jax import lax
from jax.sharding import Mesh
from jax.sharding import PartitionSpec as P

S = 4
BLK = ("blk_0", "blk_1", "blk_2", "blk_3")
epsilon = 1e-06


def passed_along(block, axis, distance):
    devices = range(lax.axis_size(axis))
    route = [((i - distance) % len(devices), i) for i in devices]
    return lax.ppermute(block, axis, route)


def in_blocks(x, dim, peers):
    before, after = (x.shape[:dim], x.shape[dim + 1 :])
    return jnp.moveaxis(x.reshape(*before, peers, -1, *after), dim, 0)


def sent_and_summed(x, axis, dim):
    parts = in_blocks(x, dim, lax.axis_size(axis))
    arrived = lax.all_to_all(parts, axis, split_axis=0, concat_axis=0, tiled=True)
    return arrived.astype(jnp.float32).sum(axis=0)


def sum_by_axis(x, axes, dim):
    far, near = axes
    own = sent_and_summed(in_blocks(x, dim, lax.axis_size(far)), near, dim + 1)
    return jnp.sum(
        lax.all_to_all(own.astype(jnp.bfloat16), far, 0, 0, tiled=True).astype(jnp.float32), axis=0
    )


def normalize(rows):
    squares = jnp.sum(rows * rows, axis=1, keepdims=True)
    length = jnp.sqrt(squares + epsilon)
    return (rows / length, length)


def similarity_derivative(
    picture_sample_group,
    caption_sample_group,
    similarity_multiplier,
    neighbour_distance,
    outer_dimension_size,
):
    similarity_matrix = (
        similarity_multiplier
        * lax.dot_general(
            picture_sample_group,
            caption_sample_group,
            (((1,), (1,)), ((), ())),
            preferred_element_type=jnp.float32,
        )
        + neighbour_distance
    )
    if outer_dimension_size:
        matched = lax.broadcasted_iota(
            jnp.int32, similarity_matrix.shape, 0
        ) == lax.broadcasted_iota(jnp.int32, similarity_matrix.shape, 1)
        match_polarity = jnp.where(matched, 1.0, -1.0).astype(jnp.float32)
    else:
        match_polarity = -jnp.ones(similarity_matrix.shape, jnp.float32)
    return (
        -similarity_multiplier
        * match_polarity
        * jax.nn.sigmoid(-match_polarity * similarity_matrix)
    ).astype(jnp.bfloat16)


def project_back(grad, unit_rows, length):
    return (grad - unit_rows * jnp.sum(unit_rows * grad, axis=1, keepdims=True)) / length


def on_device(image_features, head_weight, text_embeds, natural_exponent_factor, logit_bias):
    full_weight = lax.all_gather(head_weight, BLK, axis=0, tiled=True)
    embedded = jnp.dot(image_features, full_weight, preferred_element_type=jnp.float32)
    image_unit, image_length = normalize(embedded)
    picture_embedding_mapped = image_unit.astype(jnp.bfloat16)
    text_unit, text_length = normalize(text_embeds.astype(jnp.float32))
    text_low = text_unit.astype(jnp.bfloat16)
    similarity_multiplier = jnp.exp(natural_exponent_factor[0])
    neighbour_distance = logit_bias[0]
    image_grad = jnp.zeros(image_unit.shape, jnp.float32)
    current_neighbour_tile = text_low
    for partition_portion in range(S):
        mapping_matrix = similarity_derivative(
            picture_embedding_mapped,
            current_neighbour_tile,
            similarity_multiplier,
            neighbour_distance,
            partition_portion == 0,
        )
        image_grad = image_grad + jnp.dot(
            mapping_matrix, current_neighbour_tile, preferred_element_type=jnp.float32
        )
        if partition_portion + 1 < S:
            current_neighbour_tile = passed_along(current_neighbour_tile, BLK, -1)
    text_grad = jnp.zeros(text_unit.shape, jnp.float32)
    passing = picture_embedding_mapped
    for partition_portion in range(S):
        mapping_matrix = similarity_derivative(
            passing, text_low, similarity_multiplier, neighbour_distance, partition_portion == 0
        )
        text_grad = text_grad + lax.dot_general(
            mapping_matrix, passing, (((0,), (0,)), ((), ())), preferred_element_type=jnp.float32
        )
        if partition_portion + 1 < S:
            passing = passed_along(passing, BLK, 1)
    embed_grad = project_back(image_grad, image_unit, image_length).astype(jnp.bfloat16)
    grad_text = project_back(text_grad, text_unit, text_length).astype(jnp.bfloat16)
    grad_features = lax.dot_general(
        embed_grad, full_weight, (((1,), (1,)), ((), ())), preferred_element_type=jnp.float32
    ).astype(jnp.bfloat16)
    grad_weight = sum_by_axis(
        lax.dot_general(
            image_features, embed_grad, (((0,), (0,)), ((), ())), preferred_element_type=jnp.float32
        ).astype(jnp.bfloat16),
        (("blk_0", "blk_1"), ("blk_2", "blk_3")),
        0,
    )
    return (grad_features, grad_text, grad_weight)


def solution(mesh):
    finer = Mesh(mesh.devices.reshape(4, 8, 4, 2), ("blk_0", "blk_1", "blk_2", "blk_3"))
    return jax.shard_map(
        on_device,
        mesh=finer,
        in_specs=(P(BLK, None), P(BLK, None), P(BLK, None), P(), P()),
        out_specs=(P(BLK, None), P(BLK, None), P(BLK, None)),
        check_vma=False,
    )
```

profile of v0, /device:TPU:37, one launch (start us, length us, event | category | flops | bytes accessed | tf_op | source)
XLA Modules:
  0.0 280.2 jit_solution(11349202122939430246)
XLA Ops:
  11.2 8.6 %collective-permute-done = bf16[256,1152]{1,0:T(8,128)(2,1)S(1)} collective-permute-done((bf16[256,1152]{1,0:T(8,128)(2,1)S(1)}, bf16[256,1152]{1,0:T(8,128)(2,1)S(1)}, u32[]{:S(2)}, u32[]{:S(2)}) %collective-permute-start) | collective-permute-done | bytes 589856 | tf_op jit(solution)/shard_map/ppermute | solution.py:15
  21.2 8.1 %collective-permute-done.1 = bf16[256,1152]{1,0:T(8,128)(2,1)} collective-permute-done((bf16[256,1152]{1,0:T(8,128)(2,1)S(1)}, bf16[256,1152]{1,0:T(8,128)(2,1)}, u32[]{:S(2)}, u32[]{:S(2)}) %collective-permute-start.1) | collective-permute-done | bytes 589856 | tf_op jit(solution)/shard_map/ppermute | solution.py:15
  29.3 100.3 %all-gather.3.cloned.1.call-done = bf16[256,6,1152]{2,1,0:T(8,128)(2,1)} async-done(((bf16[1,6,1152]{2,1,0:T(8,128)(2,1)}), bf16[256,6,1152]{2,1,0:T(8,128)(2,1)}) %all-gather.3.cloned.1.call-update) | async-done | bytes 3538960 | tf_op jit(solution)/shard_map/all_gather | solution.py:79
  129.6 6.8 %reshape.22 = bf16[1536,1152]{1,0:T(8,128)(2,1)} reshape(bf16[256,6,1152]{2,1,0:T(8,128)(2,1)} %all-gather.3.cloned.1.call-done) | data formatting | bytes 7077888
  136.4 3.3 %multiply_reduce_fusion.2 = (f32[256]{0:T(256)S(1)}, f32[256,1152]{1,0:T(8,128)S(1)}) fusion(bf16[256,1536]{1,0:T(8,128)(2,1)S(1)} %copy-done, bf16[1536,1152]{1,0:T(8,128)(2,1)} %reshape.22), kind=kOutput, calls=%fused_computation.17 | convolution fusion | flops 906559232 | bytes 5506048 | tf_op jit(solution)/shard_map/dot_general | solution.py:80
  142.2 2.6 convolution_add_fusion.5
  144.7 3.2 %convolution_add_fusion.4 = f32[256,1152]{1,0:T(8,128)} fusion(f32[256,1152]{1,0:T(8,128)S(1)} %convolution_add_fusion.5, bf16[256,1152]{1,0:T(8,128)(2,1)} %collective-permute-done.1, bf16[256,1152]{1,0:T(8,128)(2,1)S(1)} %fusion.83, f32[]{:T(128)S(6)} %mul.119, f32[]{:T(128)} %bitcast.39, f32[]{:T(128)} %bitcast), kind=kOutput, calls=%fused_computation.6 | convolution fusion | flops 302743552 | bytes 3538956 | tf_op jit(solution)/shard_map/dot_general | solution.py:97
  148.0 4.1 %multiply_reduce_fusion.1 = (f32[256]{0:T(256)S(1)}, f32[256,1152]{1,0:T(8,128)}) fusion(f32[256,1152]{1,0:T(8,128)} %copy-done.4, f32[256]{0:T(256)S(1)} %add_sqrt_fusion.1, f32[256,1152]{1,0:T(8,128)} %convolution_add_fusion.4, bf16[256,1152]{1,0:T(8,128)(2,1)} %collective-permute-done.2, bf16[256,1152]{1,0:T(8,128)(2,1)S(1)} %fusion.83, f32[]{:T(128)S(6)} %mul.119, ...), kind=kOutput, calls=%fused_computation.16 | convolution fusion | flops 303628032 | bytes 4720652 | tf_op jit(solution)/shard_map/dot_general | solution.py:97
  152.0 4.3 %fusion = bf16[1536,1152]{0,1:T(8,128)(2,1)} fusion(bf16[256,1536]{1,0:T(8,128)(2,1)S(1)} %copy-done, f32[256,1152]{1,0:T(8,128)} %get-tuple-element.6, f32[256]{0:T(256)S(1)} %get-tuple-element.5, f32[256]{0:T(256)S(1)} %add_sqrt_fusion.1, f32[256,1152]{1,0:T(8,128)S(1)} %copy-done.5), kind=kOutput, calls=%fused_computation.1 | convolution fusion | flops 909213696 | bytes 6686720 | tf_op jit(solution)/shard_map/dot_general | solution.py:119
  156.3 5.8 %copy.13 = bf16[1536,1152]{1,0:T(8,128)(2,1)} copy(bf16[1536,1152]{0,1:T(8,128)(2,1)} %fusion) | data formatting | bytes 7077888 | tf_op jit(solution)/shard_map/convert_element_type | solution.py:121
  162.2 6.7 %reshape_reshape.3 = bf16[32,8,6,1152]{3,2,1,0:T(8,128)(2,1)} reshape(bf16[1536,1152]{1,0:T(8,128)(2,1)} %copy.13) | data formatting | bytes 7077888 | tf_op jit(solution)/shard_map/reshape;reshape | solution.py:20
  168.8 6.2 %copy.14 = bf16[8,32,6,1152]{3,1,2,0:T(8,128)(2,1)} copy(bf16[8,32,6,1152]{3,2,0,1:T(8,128)(2,1)} %bitcast.41) | data formatting | bytes 7077888 | tf_op jit(solution)/shard_map/transpose | solution.py:20
  175.0 4.9 %all-to-all-start = ((bf16[8,32,6,1152]{3,1,2,0:T(8,128)(2,1)}), bf16[8,32,6,1152]{3,1,2,0:T(8,128)(2,1)}, u32[]{:S(2)}, u32[]{:S(2)}) async-start(bf16[8,32,6,1152]{3,1,2,0:T(8,128)(2,1)} %copy.14), calls=%async_computation | async-start | bytes 7077888 | tf_op jit(solution)/shard_map/all_to_all | solution.py:25
  182.4 42.4 %collective-permute-done.3 = bf16[256,1152]{1,0:T(8,128)(2,1)S(1)} collective-permute-done((bf16[256,1152]{1,0:T(8,128)(2,1)S(1)}, bf16[256,1152]{1,0:T(8,128)(2,1)S(1)}, u32[]{:S(2)}, u32[]{:S(2)}) %collective-permute-start.3) | collective-permute-done | bytes 589856 | tf_op jit(solution)/shard_map/ppermute | solution.py:15
  224.8 2.5 collective-permute-start.4
  227.3 4.5 %convolution_convert_fusion.1 = bf16[256,1536]{1,0:T(8,128)(2,1)} fusion(bf16[1536,1152]{1,0:T(8,128)(2,1)} %reshape.22, f32[256,1152]{1,0:T(8,128)} %get-tuple-element.6, f32[256]{0:T(256)S(1)} %get-tuple-element.5, f32[256]{0:T(256)S(1)} %add_sqrt_fusion.1, f32[256,1152]{1,0:T(8,128)S(1)} %copy-done.6), kind=kOutput, calls=%fused_computation.8 | convolution fusion | flops 907837440 | bytes 6686720 | tf_op jit(solution)/shard_map/dot_general | solution.py:115
  231.8 2.3 collective-permute-done.4
  234.1 2.5 collective-permute-start.5
  236.6 2.7 convolution_add_fusion.2
  241.3 2.5 reduce_sum.61
  244.9 9.5 %all-to-all-start.1 = ((bf16[32,6,1152]{2,1,0:T(8,128)(2,1)}), bf16[32,6,1152]{2,1,0:T(8,128)(2,1)S(1)}, u32[]{:S(2)}, u32[]{:S(2)}) async-start(bf16[32,6,1152]{2,1,0:T(8,128)(2,1)} %copy.15), calls=%async_computation.1 | async-start | bytes 1179648 | tf_op jit(solution)/shard_map/all_to_all | solution.py:33
  254.4 3.7 %multiply_reduce_fusion = (f32[256]{0:T(256)S(1)}, f32[256,1152]{1,0:T(8,128)}) fusion(f32[256]{0:T(256)S(1)} %add_sqrt_fusion, bf16[256,1152]{1,0:T(8,128)(2,1)S(1)} %copy-done.1, f32[256,1152]{1,0:T(8,128)} %convolution_add_fusion.1, bf16[256,1152]{1,0:T(8,128)(2,1)} %collective-permute-done.5, bf16[256,1152]{1,0:T(8,128)(2,1)S(1)} %fusion.82, ...), kind=kOutput, calls=%fused_computation.14 | convolution fusion | flops 303922944 | bytes 4130828 | tf_op jit(solution)/shard_map/dot_general | solution.py:108
  258.1 2.4 divide_convert_fusion
  260.5 12.2 %all-to-all-done.1 = bf16[32,6,1152]{2,1,0:T(8,128)(2,1)S(1)} async-done(((bf16[32,6,1152]{2,1,0:T(8,128)(2,1)}), bf16[32,6,1152]{2,1,0:T(8,128)(2,1)S(1)}, u32[]{:S(2)}, u32[]{:S(2)}) %all-to-all-start.1) | async-done | bytes 442400 | tf_op jit(solution)/shard_map/all_to_all | solution.py:33
  (34 shorter events, 12.9 us)
Async XLA Ops:
  7.2 129.2 %copy-start = (bf16[256,1536]{1,0:T(8,128)(2,1)S(1)}, bf16[256,1536]{1,0:T(8,128)(2,1)}, u32[]{:S(2)}) copy-start(bf16[256,1536]{1,0:T(8,128)(2,1)} %param.5) | copy-start | bytes 2359300
  7.2 122.4 %all-gather.3.cloned.1.call-start = ((), (), s32[]{:S(2)}) async-start(), calls=%async_computation.2 | async-start | bytes 4737024 | tf_op jit(solution)/shard_map/all_gather | solution.py:79
  10.5 9.4 %collective-permute-start = (bf16[256,1152]{1,0:T(8,128)(2,1)S(1)}, bf16[256,1152]{1,0:T(8,128)(2,1)S(1)}, u32[]{:S(2)}, u32[]{:S(2)}) collective-permute-start(bf16[256,1152]{1,0:T(8,128)(2,1)S(1)} %fusion.82), channel_id=1, source_target_pairs={{1,0},{2,1},{3,2},{4,3},{5,4},{6,5},{7,6},{8,7},{9,8},{10,9},{11,1... | collective-permute-start | bytes 1769480 | tf_op jit(solution)/shard_map/ppermute | solution.py:15
  19.9 116.5 %copy-start.2 = (bf16[256,1152]{1,0:T(8,128)(2,1)}, bf16[256,1152]{1,0:T(8,128)(2,1)S(1)}, u32[]{:S(2)}) copy-start(bf16[256,1152]{1,0:T(8,128)(2,1)S(1)} %collective-permute-done) | copy-start | bytes 1769476
  19.9 9.4 %collective-permute-start.1 = (bf16[256,1152]{1,0:T(8,128)(2,1)S(1)}, bf16[256,1152]{1,0:T(8,128)(2,1)}, u32[]{:S(2)}, u32[]{:S(2)}) collective-permute-start(bf16[256,1152]{1,0:T(8,128)(2,1)S(1)} %collective-permute-done), channel_id=1, source_target_pairs={{1,0},{2,1},{3,2},{4,3},{5,4},{6,5},{7,6},{8,7},{9,8},{10,9},{11,1... | collective-permute-start | bytes 1769480 | tf_op jit(solution)/shard_map/ppermute | solution.py:15
  29.3 118.7 %collective-permute-start.2 = (bf16[256,1152]{1,0:T(8,128)(2,1)}, bf16[256,1152]{1,0:T(8,128)(2,1)}, u32[]{:S(2)}, u32[]{:S(2)}) collective-permute-start(bf16[256,1152]{1,0:T(8,128)(2,1)} %collective-permute-done.1), channel_id=1, source_target_pairs={{1,0},{2,1},{3,2},{4,3},{5,4},{6,5},{7,6},{8,7},{9,8},{10,9},{11,1... | collective-permute-start | bytes 1769480 | tf_op jit(solution)/shard_map/ppermute | solution.py:15
  139.7 1.1 copy-start.4
  148.0 4.1 %copy-start.5 = (f32[256,1152]{1,0:T(8,128)S(1)}, f32[256,1152]{1,0:T(8,128)}, u32[]{:S(2)}) copy-start(f32[256,1152]{1,0:T(8,128)} %copy-done.4) | copy-start | bytes 3538948
  175.0 66.3 %all-to-all-start = ((bf16[8,32,6,1152]{3,1,2,0:T(8,128)(2,1)}), bf16[8,32,6,1152]{3,1,2,0:T(8,128)(2,1)}, u32[]{:S(2)}, u32[]{:S(2)}) async-start(bf16[8,32,6,1152]{3,1,2,0:T(8,128)(2,1)} %copy.14), calls=%async_computation | async-start | bytes 7077888 | tf_op jit(solution)/shard_map/all_to_all | solution.py:25
  179.9 47.4 %copy-start.6 = (f32[256,1152]{1,0:T(8,128)S(1)}, f32[256,1152]{1,0:T(8,128)}, u32[]{:S(2)}) copy-start(f32[256,1152]{1,0:T(8,128)} %copy-done.4) | copy-start | bytes 3538948
  179.9 45.0 %collective-permute-start.3 = (bf16[256,1152]{1,0:T(8,128)(2,1)S(1)}, bf16[256,1152]{1,0:T(8,128)(2,1)S(1)}, u32[]{:S(2)}, u32[]{:S(2)}) collective-permute-start(bf16[256,1152]{1,0:T(8,128)(2,1)S(1)} %fusion.83), channel_id=1, source_target_pairs={{255,0},{0,1},{1,2},{2,3},{3,4},{4,5},{5,6},{6,7},{7,8},{8,9},{9,1... | collective-permute-start | bytes 1769480 | tf_op jit(solution)/shard_map/ppermute | solution.py:15
  224.8 7.0 %copy-start.3 = (bf16[256,1152]{1,0:T(8,128)(2,1)}, bf16[256,1152]{1,0:T(8,128)(2,1)S(1)}, u32[]{:S(2)}) copy-start(bf16[256,1152]{1,0:T(8,128)(2,1)S(1)} %collective-permute-done.3) | copy-start | bytes 1769476
  224.8 9.3 %collective-permute-start.4 = (bf16[256,1152]{1,0:T(8,128)(2,1)S(1)}, bf16[256,1152]{1,0:T(8,128)(2,1)S(1)}, u32[]{:S(2)}, u32[]{:S(2)}) collective-permute-start(bf16[256,1152]{1,0:T(8,128)(2,1)S(1)} %collective-permute-done.3), channel_id=1, source_target_pairs={{255,0},{0,1},{1,2},{2,3},{3,4},{4,5},{5,6},{6,7},{7,8},{8,9},{9,1... | collective-permute-start | bytes 1769480 | tf_op jit(solution)/shard_map/ppermute | solution.py:15
  234.1 20.2 %collective-permute-start.5 = (bf16[256,1152]{1,0:T(8,128)(2,1)S(1)}, bf16[256,1152]{1,0:T(8,128)(2,1)}, u32[]{:S(2)}, u32[]{:S(2)}) collective-permute-start(bf16[256,1152]{1,0:T(8,128)(2,1)S(1)} %collective-permute-done.4), channel_id=1, source_target_pairs={{255,0},{0,1},{1,2},{2,3},{3,4},{4,5},{5,6},{6,7},{7,8},{8,9},{9,1... | collective-permute-start | bytes 1769480 | tf_op jit(solution)/shard_map/ppermute | solution.py:15
  243.9 10.5 %copy-start.1 = (bf16[256,1152]{1,0:T(8,128)(2,1)S(1)}, bf16[256,1152]{1,0:T(8,128)(2,1)}, u32[]{:S(2)}) copy-start(bf16[256,1152]{1,0:T(8,128)(2,1)} %param.7) | copy-start | bytes 1769476
  244.9 27.8 %all-to-all-start.1 = ((bf16[32,6,1152]{2,1,0:T(8,128)(2,1)}), bf16[32,6,1152]{2,1,0:T(8,128)(2,1)S(1)}, u32[]{:S(2)}, u32[]{:S(2)}) async-start(bf16[32,6,1152]{2,1,0:T(8,128)(2,1)} %copy.15), calls=%async_computation.1 | async-start | bytes 1179648 | tf_op jit(solution)/shard_map/all_to_all | solution.py:33
Sparse Core Ops, SparseCore 0:
  11.8 117.7 all-gather.2
where the time goes:
time: 281 us; the launch traced here: 280 us
  waiting for transfers between devices  175 us (62%)
  matrix products  33.6 us (12%)
  local copies, waits for them, and re-layouts  26.9 us (10%)
  starting transfers between devices  21.3 us (8%)
  between operations  15.5 us (6%)
  other arithmetic  8.36 us (3%)
    all_gather x1, waiting for transfers between devices, on_device(): full_weight = lax.all_gather(head_weight, BLK, axis=0, tiled=True)  100 us
    ppermute x6, waiting for transfers between devices, passed_along(): return lax.ppermute(block, axis, route)  61.4 us
    all_to_all x1, waiting for transfers between devices, sum_by_axis(): lax.all_to_all(own.astype(jnp.bfloat16), far, 0, 0, tiled=True)  12.2 us
    dot_general x4, matrix products, on_device(): jnp.dot(mapping_matrix, current_neighbour_tile, preferred_element_type=jn...  11.3 us
    dot_general x4, matrix products, on_device(): lax.dot_general(mapping_matrix, passing, (((0,), (0,)), ((), ())), prefer...  9.82 us
    all_to_all x1, starting transfers between devices, sum_by_axis(): lax.all_to_all(own.astype(jnp.bfloat16), far, 0, 0, tiled=True)  9.49 us
    unnamed x15, local copies, waits for them, and re-layouts  7.29 us
    ppermute x6, starting transfers between devices, passed_along(): return lax.ppermute(block, axis, route)  6.89 us
  transfers between devices with their start and end apart: 9, of which 6 were waited for; matrix products, arithmetic and copies ran while one was open for 14% of the time, Pallas kernels for 0%

commit v1 on v0

--- a/solution.py
+++ b/solution.py
@@ -3,6 +3,7 @@
 from jax import lax
 from jax.sharding import Mesh
 from jax.sharding import PartitionSpec as P
+from jax.lax import all_to_all, axis_size
 
 S = 4
 BLK = ("blk_0", "blk_1", "blk_2", "blk_3")
@@ -76,7 +77,9 @@
 
 
 def on_device(image_features, head_weight, text_embeds, natural_exponent_factor, logit_bias):
-    full_weight = lax.all_gather(head_weight, BLK, axis=0, tiled=True)
+    full_weight = jnp.concatenate(
+        all_to_all(jnp.stack([head_weight] * axis_size(BLK), axis=0), BLK, 0, 0), axis=0
+    )
     embedded = jnp.dot(image_features, full_weight, preferred_element_type=jnp.float32)
     image_unit, image_length = normalize(embedded)
     picture_embedding_mapped = image_unit.astype(jnp.bfloat16)

time: 281 us -> 293 us (1.043)
  starting transfers between devices: 21.3 us -> 54.5 us
  between operations: 15.5 us -> 2.07 us
  waiting for transfers between devices: 175 us -> 162 us
  local copies, waits for them, and re-layouts: 26.9 us -> 30.1 us
  matrix products: 33.6 us -> 36.8 us
    all_gather x1 -> x0, waiting for transfers between devices: 100 us -> none  [on_device(): full_weight = lax.all_gather(head_weight, BLK, axis=0, tiled=True)]
    all_to_all x0 -> x1, waiting for transfers between devices: none -> 68.7 us  [on_device(): all_to_all(jnp.stack([head_weight] * axis_size(BLK), axis=0), BLK, 0, 0)]
    ppermute x6, waiting for transfers between devices: 61.4 us -> 81.6 us  [passed_along(): return lax.ppermute(block, axis, route)]
    all_to_all x1, starting transfers between devices: 4.86 us -> 20.6 us  [sent_and_summed(): lax.all_to_all(parts, axis, split_axis=0, concat_axis=0, tiled=True)]
    all_to_all x0 -> x1, starting transfers between devices: none -> 15.5 us  [on_device(): all_to_all(jnp.stack([head_weight] * axis_size(BLK), axis=0), BLK, 0, 0)]
    unnamed x15 -> x8, local copies, waits for them, and re-layouts: 7.29 us -> 0.49 us
    reshape x0 -> x1, local copies, waits for them, and re-layouts: none -> 6.77 us  [on_device(): jnp.concatenate(all_to_all(jnp.stack([head_weight] * axis_size(BLK), axis...]
    another operation x0 -> x1, local copies, waits for them, and re-layouts: none -> 3.29 us  [on_device(): jnp.stack([head_weight] * axis_size(BLK), axis=0)]
where the time goes in v1:
time: 293 us; the launch traced here: 292 us
  waiting for transfers between devices  162 us (55%)
  starting transfers between devices  54.5 us (19%)
  matrix products  36.8 us (13%)
  local copies, waits for them, and re-layouts  30.1 us (10%)
  other arithmetic  6.24 us (2%)
    ppermute x6, waiting for transfers between devices, passed_along(): return lax.ppermute(block, axis, route)  81.6 us
    all_to_all x1, waiting for transfers between devices, on_device(): all_to_all(jnp.stack([head_weight] * axis_size(BLK), axis=0), BLK, 0, 0)  68.7 us
    all_to_all x1, starting transfers between devices, sent_and_summed(): lax.all_to_all(parts, axis, split_axis=0, concat_axis=0, tiled=True)  20.6 us
    all_to_all x1, starting transfers between devices, on_device(): all_to_all(jnp.stack([head_weight] * axis_size(BLK), axis=0), BLK, 0, 0)  15.5 us
    dot_general x4, matrix products, on_device(): jnp.dot(mapping_matrix, current_neighbour_tile, preferred_element_type=jn...  12.3 us
    all_to_all x1, waiting for transfers between devices, sum_by_axis(): lax.all_to_all(own.astype(jnp.bfloat16), far, 0, 0, tiled=True)  12.2 us
    all_to_all x1, starting transfers between devices, sum_by_axis(): lax.all_to_all(own.astype(jnp.bfloat16), far, 0, 0, tiled=True)  11.8 us
    dot_general x4, matrix products, on_device(): lax.dot_general(mapping_matrix, passing, (((0,), (0,)), ((), ())), prefer...  11.7 us
  transfers between devices with their start and end apart: 9, of which 6 were waited for; matrix products, arithmetic and copies ran while one was open for 14% of the time, Pallas kernels for 0%

profile of v1, /device:TPU:37, one launch (start us, length us, event | category | flops | bytes accessed | tf_op | source)
XLA Modules:
  0.0 292.1 jit_solution(4390223563263706028)
XLA Ops:
  0.6 3.3 %stack.2 = bf16[256,6,1152]{2,1,0:T(8,128)(2,1)} broadcast(bf16[6,1152]{1,0:T(8,128)(2,1)} %param.6), dimensions={1,2} | broadcast | bytes 3552768 | tf_op jit(solution)/shard_map/stack | solution.py:81
  3.9 15.5 %all-to-all-start = ((bf16[256,6,1152]{2,1,0:T(8,128)(2,1)}), bf16[256,6,1152]{2,1,0:T(8,128)(2,1)}, u32[]{:S(2)}, u32[]{:S(2)}) async-start(bf16[256,6,1152]{2,1,0:T(8,128)(2,1)} %stack.2), calls=%async_computation | async-start | bytes 9437184 | tf_op jit(solution)/shard_map/all_to_all | solution.py:81
  20.4 21.6 %collective-permute-done = bf16[256,1152]{1,0:T(8,128)(2,1)S(1)} collective-permute-done((bf16[256,1152]{1,0:T(8,128)(2,1)S(1)}, bf16[256,1152]{1,0:T(8,128)(2,1)S(1)}, u32[]{:S(2)}, u32[]{:S(2)}) %collective-permute-start) | collective-permute-done | bytes 589856 | tf_op jit(solution)/shard_map/ppermute | solution.py:16
  43.3 13.9 %collective-permute-done.1 = bf16[256,1152]{1,0:T(8,128)(2,1)} collective-permute-done((bf16[256,1152]{1,0:T(8,128)(2,1)S(1)}, bf16[256,1152]{1,0:T(8,128)(2,1)}, u32[]{:S(2)}, u32[]{:S(2)}) %collective-permute-start.1) | collective-permute-done | bytes 589856 | tf_op jit(solution)/shard_map/ppermute | solution.py:16
  57.2 68.7 %all-to-all-done = bf16[256,6,1152]{2,1,0:T(8,128)(2,1)} async-done(((bf16[256,6,1152]{2,1,0:T(8,128)(2,1)}), bf16[256,6,1152]{2,1,0:T(8,128)(2,1)}, u32[]{:S(2)}, u32[]{:S(2)}) %all-to-all-start) | async-done | bytes 3538976 | tf_op jit(solution)/shard_map/all_to_all | solution.py:81
  125.9 6.8 %reshape.26 = bf16[1536,1152]{1,0:T(8,128)(2,1)} reshape(bf16[256,6,1152]{2,1,0:T(8,128)(2,1)} %all-to-all-done) | data formatting | bytes 7077888 | tf_op jit(solution)/shard_map/reshape | solution.py:80
  132.7 3.3 %multiply_reduce_fusion.2 = (f32[256]{0:T(256)S(1)}, f32[256,1152]{1,0:T(8,128)S(1)}) fusion(bf16[256,1536]{1,0:T(8,128)(2,1)S(1)} %copy-done, bf16[1536,1152]{1,0:T(8,128)(2,1)} %reshape.26), kind=kOutput, calls=%fused_computation.17 | convolution fusion | flops 906559232 | bytes 5506048 | tf_op jit(solution)/shard_map/dot_general | solution.py:83
  138.4 3.3 %convolution_add_fusion.5 = f32[256,1152]{1,0:T(8,128)} fusion(f32[256,1152]{1,0:T(8,128)} %fusion.84, bf16[256,1152]{1,0:T(8,128)(2,1)S(1)} %collective-permute-done, bf16[256,1152]{1,0:T(8,128)(2,1)S(1)} %fusion.83, f32[]{:T(128)S(6)} %mul.119, f32[]{:T(128)} %bitcast.39, f32[]{:T(128)} %bitcast), kind=kOutput, calls=%fused_computation.7 | convolution fusion | flops 302743552 | bytes 3538956 | tf_op jit(solution)/shard_map/dot_general | solution.py:100
  141.7 3.6 %convolution_add_fusion.4 = f32[256,1152]{1,0:T(8,128)} fusion(f32[256,1152]{1,0:T(8,128)} %convolution_add_fusion.5, bf16[256,1152]{1,0:T(8,128)(2,1)} %collective-permute-done.1, bf16[256,1152]{1,0:T(8,128)(2,1)S(1)} %fusion.83, f32[]{:T(128)S(6)} %mul.119, f32[]{:T(128)} %bitcast.38, f32[]{:T(128)} %bitcast), kind=kOutput, calls=%fused_computation.6 | convolution fusion | flops 302743552 | bytes 3538956 | tf_op jit(solution)/shard_map/dot_general | solution.py:100
  145.3 4.0 %multiply_reduce_fusion.1 = (f32[256]{0:T(256)S(1)}, f32[256,1152]{1,0:T(8,128)}) fusion(f32[256,1152]{1,0:T(8,128)} %copy-done.2, f32[256]{0:T(256)S(1)} %add_sqrt_fusion.1, f32[256,1152]{1,0:T(8,128)} %convolution_add_fusion.4, bf16[256,1152]{1,0:T(8,128)(2,1)} %collective-permute-done.2, bf16[256,1152]{1,0:T(8,128)(2,1)S(1)} %fusion.83, f32[]{:T(128)S(6)} %mul.119, ...), kind=kOutput, calls=%fused_computation.16 | convolution fusion | flops 303628032 | bytes 4720652 | tf_op jit(solution)/shard_map/dot_general | solution.py:100
  149.3 4.7 %fusion = bf16[1536,1152]{0,1:T(8,128)(2,1)} fusion(bf16[256,1536]{1,0:T(8,128)(2,1)S(1)} %copy-done, f32[256,1152]{1,0:T(8,128)} %get-tuple-element.6, f32[256]{0:T(256)S(1)} %get-tuple-element.5, f32[256]{0:T(256)S(1)} %add_sqrt_fusion.1, f32[256,1152]{1,0:T(8,128)} %copy-done.2), kind=kOutput, calls=%fused_computation.1 | convolution fusion | flops 909213696 | bytes 6686720 | tf_op jit(solution)/shard_map/dot_general | solution.py:122
  153.9 5.8 %copy.13 = bf16[1536,1152]{1,0:T(8,128)(2,1)} copy(bf16[1536,1152]{0,1:T(8,128)(2,1)} %fusion) | data formatting | bytes 7077888 | tf_op jit(solution)/shard_map/convert_element_type | solution.py:124
  159.7 6.7 %reshape_reshape.3 = bf16[32,8,6,1152]{3,2,1,0:T(8,128)(2,1)} reshape(bf16[1536,1152]{1,0:T(8,128)(2,1)} %copy.13) | data formatting | bytes 7077888 | tf_op jit(solution)/shard_map/reshape;reshape | solution.py:21
  166.4 6.2 %copy.14 = bf16[8,32,6,1152]{3,1,2,0:T(8,128)(2,1)} copy(bf16[8,32,6,1152]{3,2,0,1:T(8,128)(2,1)} %bitcast.40) | data formatting | bytes 7077888 | tf_op jit(solution)/shard_map/transpose | solution.py:21
  172.6 20.6 %all-to-all-start.1 = ((bf16[8,32,6,1152]{3,1,2,0:T(8,128)(2,1)}), bf16[8,32,6,1152]{3,1,2,0:T(8,128)(2,1)}, u32[]{:S(2)}, u32[]{:S(2)}) async-start(bf16[8,32,6,1152]{3,1,2,0:T(8,128)(2,1)} %copy.14), calls=%async_computation.1 | async-start | bytes 7077888 | tf_op jit(solution)/shard_map/all_to_all | solution.py:26
  195.7 43.7 %collective-permute-done.3 = bf16[256,1152]{1,0:T(8,128)(2,1)S(1)} collective-permute-done((bf16[256,1152]{1,0:T(8,128)(2,1)S(1)}, bf16[256,1152]{1,0:T(8,128)(2,1)S(1)}, u32[]{:S(2)}, u32[]{:S(2)}) %collective-permute-start.3) | collective-permute-done | bytes 589856 | tf_op jit(solution)/shard_map/ppermute | solution.py:16
  239.5 2.5 collective-permute-start.4
  241.9 4.5 %convolution_convert_fusion.1 = bf16[256,1536]{1,0:T(8,128)(2,1)} fusion(bf16[1536,1152]{1,0:T(8,128)(2,1)} %reshape.26, f32[256,1152]{1,0:T(8,128)} %get-tuple-element.6, f32[256]{0:T(256)S(1)} %get-tuple-element.5, f32[256]{0:T(256)S(1)} %add_sqrt_fusion.1, f32[256,1152]{1,0:T(8,128)S(1)} %copy-done.3), kind=kOutput, calls=%fused_computation.8 | convolution fusion | flops 907837440 | bytes 6686720 | tf_op jit(solution)/shard_map/dot_general | solution.py:118
  251.2 3.3 %convolution_add_fusion.2 = f32[256,1152]{1,0:T(8,128)} fusion(f32[256,1152]{1,0:T(8,128)} %fusion.85, bf16[256,1152]{1,0:T(8,128)(2,1)S(1)} %collective-permute-done.3, bf16[256,1152]{1,0:T(8,128)(2,1)S(1)} %fusion.82, f32[]{:T(128)S(6)} %mul.119, f32[]{:T(128)} %bitcast.36, f32[]{:T(128)} %bitcast), kind=kOutput, calls=%fused_computation.4 | convolution fusion | flops 302743552 | bytes 3538956 | tf_op jit(solution)/shard_map/dot_general | solution.py:111
  254.6 3.3 %convolution_add_fusion.1 = f32[256,1152]{1,0:T(8,128)} fusion(f32[256,1152]{1,0:T(8,128)} %convolution_add_fusion.2, bf16[256,1152]{1,0:T(8,128)(2,1)S(1)} %collective-permute-done.4, bf16[256,1152]{1,0:T(8,128)(2,1)S(1)} %fusion.82, f32[]{:T(128)S(6)} %mul.119, f32[]{:T(128)} %bitcast.35, f32[]{:T(128)} %bitcast), kind=kOutput, calls=%fused_computation.3 | convolution fusion | flops 302743552 | bytes 3538956 | tf_op jit(solution)/shard_map/dot_general | solution.py:111
  257.9 2.5 reduce_sum.61
  261.4 11.8 %all-to-all-start.2 = ((bf16[32,6,1152]{2,1,0:T(8,128)(2,1)}), bf16[32,6,1152]{2,1,0:T(8,128)(2,1)S(1)}, u32[]{:S(2)}, u32[]{:S(2)}) async-start(bf16[32,6,1152]{2,1,0:T(8,128)(2,1)} %copy.15), calls=%async_computation.2 | async-start | bytes 1179648 | tf_op jit(solution)/shard_map/all_to_all | solution.py:34
  273.1 3.7 %multiply_reduce_fusion = (f32[256]{0:T(256)S(1)}, f32[256,1152]{1,0:T(8,128)}) fusion(f32[256]{0:T(256)S(1)} %add_sqrt_fusion, bf16[256,1152]{1,0:T(8,128)(2,1)S(1)} %copy-done.1, f32[256,1152]{1,0:T(8,128)} %convolution_add_fusion.1, bf16[256,1152]{1,0:T(8,128)(2,1)} %collective-permute-done.5, bf16[256,1152]{1,0:T(8,128)(2,1)S(1)} %fusion.82, ...), kind=kOutput, calls=%fused_computation.14 | convolution fusion | flops 303922944 | bytes 4130828 | tf_op jit(solution)/shard_map/dot_general | solution.py:111
  279.2 12.2 %all-to-all-done.2 = bf16[32,6,1152]{2,1,0:T(8,128)(2,1)S(1)} async-done(((bf16[32,6,1152]{2,1,0:T(8,128)(2,1)}), bf16[32,6,1152]{2,1,0:T(8,128)(2,1)S(1)}, u32[]{:S(2)}, u32[]{:S(2)}) %all-to-all-start.2) | async-done | bytes 442400 | tf_op jit(solution)/shard_map/all_to_all | solution.py:34
  (28 shorter events, 14.8 us)
Async XLA Ops:
  0.6 132.0 %copy-start = (bf16[256,1536]{1,0:T(8,128)(2,1)S(1)}, bf16[256,1536]{1,0:T(8,128)(2,1)}, u32[]{:S(2)}) copy-start(bf16[256,1536]{1,0:T(8,128)(2,1)} %param.5) | copy-start | bytes 2359300
  3.9 15.5 %copy-start.1 = (bf16[256,1152]{1,0:T(8,128)(2,1)S(1)}, bf16[256,1152]{1,0:T(8,128)(2,1)}, u32[]{:S(2)}) copy-start(bf16[256,1152]{1,0:T(8,128)(2,1)} %param.7) | copy-start | bytes 1769476
  3.9 122.0 %all-to-all-start = ((bf16[256,6,1152]{2,1,0:T(8,128)(2,1)}), bf16[256,6,1152]{2,1,0:T(8,128)(2,1)}, u32[]{:S(2)}, u32[]{:S(2)}) async-start(bf16[256,6,1152]{2,1,0:T(8,128)(2,1)} %stack.2), calls=%async_computation | async-start | bytes 9437184 | tf_op jit(solution)/shard_map/all_to_all | solution.py:81
  19.9 22.0 %collective-permute-start = (bf16[256,1152]{1,0:T(8,128)(2,1)S(1)}, bf16[256,1152]{1,0:T(8,128)(2,1)S(1)}, u32[]{:S(2)}, u32[]{:S(2)}) collective-permute-start(bf16[256,1152]{1,0:T(8,128)(2,1)S(1)} %fusion.82), channel_id=1, source_target_pairs={{1,0},{2,1},{3,2},{4,3},{5,4},{6,5},{7,6},{8,7},{9,8},{10,9},{11,1... | collective-permute-start | bytes 1769480 | tf_op jit(solution)/shard_map/ppermute | solution.py:16
  42.0 15.2 %collective-permute-start.1 = (bf16[256,1152]{1,0:T(8,128)(2,1)S(1)}, bf16[256,1152]{1,0:T(8,128)(2,1)}, u32[]{:S(2)}, u32[]{:S(2)}) collective-permute-start(bf16[256,1152]{1,0:T(8,128)(2,1)S(1)} %collective-permute-done), channel_id=1, source_target_pairs={{1,0},{2,1},{3,2},{4,3},{5,4},{6,5},{7,6},{8,7},{9,8},{10,9},{11,1... | collective-permute-start | bytes 1769480 | tf_op jit(solution)/shard_map/ppermute | solution.py:16
  57.2 88.1 %collective-permute-start.2 = (bf16[256,1152]{1,0:T(8,128)(2,1)}, bf16[256,1152]{1,0:T(8,128)(2,1)}, u32[]{:S(2)}, u32[]{:S(2)}) collective-permute-start(bf16[256,1152]{1,0:T(8,128)(2,1)} %collective-permute-done.1), channel_id=1, source_target_pairs={{1,0},{2,1},{3,2},{4,3},{5,4},{6,5},{7,6},{8,7},{9,8},{10,9},{11,1... | collective-permute-start | bytes 1769480 | tf_op jit(solution)/shard_map/ppermute | solution.py:16
  135.9 1.1 copy-start.2
  172.6 85.3 %all-to-all-start.1 = ((bf16[8,32,6,1152]{3,1,2,0:T(8,128)(2,1)}), bf16[8,32,6,1152]{3,1,2,0:T(8,128)(2,1)}, u32[]{:S(2)}, u32[]{:S(2)}) async-start(bf16[8,32,6,1152]{3,1,2,0:T(8,128)(2,1)} %copy.14), calls=%async_computation.1 | async-start | bytes 7077888 | tf_op jit(solution)/shard_map/all_to_all | solution.py:26
  193.1 48.8 %copy-start.3 = (f32[256,1152]{1,0:T(8,128)S(1)}, f32[256,1152]{1,0:T(8,128)}, u32[]{:S(2)}) copy-start(f32[256,1152]{1,0:T(8,128)} %copy-done.2) | copy-start | bytes 3538948
  193.1 46.3 %collective-permute-start.3 = (bf16[256,1152]{1,0:T(8,128)(2,1)S(1)}, bf16[256,1152]{1,0:T(8,128)(2,1)S(1)}, u32[]{:S(2)}, u32[]{:S(2)}) collective-permute-start(bf16[256,1152]{1,0:T(8,128)(2,1)S(1)} %fusion.83), channel_id=1, source_target_pairs={{255,0},{0,1},{1,2},{2,3},{3,4},{4,5},{5,6},{6,7},{7,8},{8,9},{9,1... | collective-permute-start | bytes 1769480 | tf_op jit(solution)/shard_map/ppermute | solution.py:16
  239.5 9.3 %collective-permute-start.4 = (bf16[256,1152]{1,0:T(8,128)(2,1)S(1)}, bf16[256,1152]{1,0:T(8,128)(2,1)S(1)}, u32[]{:S(2)}, u32[]{:S(2)}) collective-permute-start(bf16[256,1152]{1,0:T(8,128)(2,1)S(1)} %collective-permute-done.3), channel_id=1, source_target_pairs={{255,0},{0,1},{1,2},{2,3},{3,4},{4,5},{5,6},{6,7},{7,8},{8,9},{9,1... | collective-permute-start | bytes 1769480 | tf_op jit(solution)/shard_map/ppermute | solution.py:16
  248.8 24.4 %collective-permute-start.5 = (bf16[256,1152]{1,0:T(8,128)(2,1)S(1)}, bf16[256,1152]{1,0:T(8,128)(2,1)}, u32[]{:S(2)}, u32[]{:S(2)}) collective-permute-start(bf16[256,1152]{1,0:T(8,128)(2,1)S(1)} %collective-permute-done.4), channel_id=1, source_target_pairs={{255,0},{0,1},{1,2},{2,3},{3,4},{4,5},{5,6},{6,7},{7,8},{8,9},{9,1... | collective-permute-start | bytes 1769480 | tf_op jit(solution)/shard_map/ppermute | solution.py:16
  261.4 30.0 %all-to-all-start.2 = ((bf16[32,6,1152]{2,1,0:T(8,128)(2,1)}), bf16[32,6,1152]{2,1,0:T(8,128)(2,1)S(1)}, u32[]{:S(2)}, u32[]{:S(2)}) async-start(bf16[32,6,1152]{2,1,0:T(8,128)(2,1)} %copy.15), calls=%async_computation.2 | async-start | bytes 1179648 | tf_op jit(solution)/shard_map/all_to_all | solution.py:34
